TPU v7x, 32 devices: a 4x4x1 block of a 4x4x8 slice. The times are simulated.
32 devices in a mesh: dp: 1 (over z), tp: 4 (over y), cp: 8 (over x, core).
Axes of the slice: x: 4, y: 4, z: 1, core: 2. Of those that a mesh axis runs over, the one named last changes fastest.
The devices are a block of a 4x4x8 slice.
Arguments:
- x: bfloat16 [8192, 4096], P(('dp', 'cp'))
- attn_gain: bfloat16 [4096], replicated
- w_q: bfloat16 [4096, 4096], P(None, 'tp')
- w_k: bfloat16 [4096, 1024], P(None, 'tp')
- w_v: bfloat16 [4096, 1024], P(None, 'tp')
- w_o: bfloat16 [4096, 4096], P('tp')
- mlp_gain: bfloat16 [4096], replicated
- w_gate: bfloat16 [4096, 14336], P(None, 'tp')
- w_up: bfloat16 [4096, 14336], P(None, 'tp')
- w_down: bfloat16 [14336, 4096], P('tp')
Outputs:
- output 1: bfloat16 [8192, 4096], P(('dp', 'cp'))
- output 2: bfloat16 [8192, 8, 128], P(('dp', 'cp'), 'tp')
- output 3: bfloat16 [8192, 8, 128], P(('dp', 'cp'), 'tp')
All inputs are finite; a program needn't handle non-finite values.
Results may differ from a plain program's by a relative error of at most 0.013606.
Values are sent between devices in bfloat16 or wider.
A program may use at most 768 MiB of HBM per device.

v0:
```python
import functools
import math
import jax
import jax.numpy as jnp
from jax import lax
from jax.experimental import pallas as pl
from jax.experimental.pallas import tpu as pltpu
from jax.sharding import PartitionSpec as P

HEAD_DIM = 128
ROPE_THETA = 1000000.0
NORM_EPS = 1e-5
MASK_VALUE = -1e30
SCORE_EXP2 = HEAD_DIM ** -0.5 * math.log2(math.e)
KEY_TILE = 1024
ROW_TILE = 256
COL_TILE = 1024
FF_TILE = 512
VMEM_LIMIT = 60 * 1024 * 1024


def rms_norm(rows, gain):
    wide = rows.astype(jnp.float32)
    inv_rms = lax.rsqrt(jnp.mean(wide * wide, axis=-1, keepdims=True) + NORM_EPS)
    return (wide * inv_rms * gain.astype(jnp.float32)).astype(jnp.bfloat16)


def rope_tables(positions):
    inv_freq = jnp.asarray(ROPE_THETA, jnp.float32) ** (-jnp.arange(0, HEAD_DIM, 2, dtype=jnp.float32) / HEAD_DIM)
    angles = positions.astype(jnp.float32)[:, None] * inv_freq[None, :]
    cos, sin = jnp.cos(angles), jnp.sin(angles)
    return jnp.concatenate([cos, cos], axis=-1), jnp.concatenate([-sin, sin], axis=-1)


def rope_head(head, cos_t, sin_t):
    wide = head.astype(jnp.bfloat16).astype(jnp.float32)
    return (wide * cos_t + pltpu.roll(wide, HEAD_DIM // 2, 1) * sin_t).astype(jnp.bfloat16)


def kv_kernel(x_ref, gain_ref, cos_ref, sin_ref, w_k_ref, w_v_ref, kv_ref):
    normed = rms_norm(x_ref[...], gain_ref[...])
    width = w_k_ref.shape[1]
    keys = jnp.dot(normed, w_k_ref[...], preferred_element_type=jnp.float32)
    for head in range(width // HEAD_DIM):
        cols = slice(head * HEAD_DIM, (head + 1) * HEAD_DIM)
        kv_ref[:, cols] = rope_head(keys[:, cols], cos_ref[...], sin_ref[...])
    kv_ref[:, width:] = jnp.dot(normed, w_v_ref[...], preferred_element_type=jnp.float32).astype(jnp.bfloat16)


def q_kernel(x_ref, gain_ref, cos_ref, sin_ref, w_q_ref, q_ref):
    normed = rms_norm(x_ref[...], gain_ref[...])
    queries = jnp.dot(normed, w_q_ref[...], preferred_element_type=jnp.float32)
    for head in range(w_q_ref.shape[1] // HEAD_DIM):
        cols = slice(head * HEAD_DIM, (head + 1) * HEAD_DIM)
        q_ref[:, cols] = rope_head(queries[:, cols], cos_ref[...], sin_ref[...])


def project(kernel, x, gain, cos_tab, sin_tab, weights, out_cols, links=None):
    rows, dim = x.shape
    row_block = lambda cols: pl.BlockSpec((ROW_TILE, cols), lambda i: (i, 0))
    w_cols = sum(w.shape[1] for w in weights)

    def body(ins, out_ref, scratch, links):
        if links:
            pl.when(pl.program_id(0) == 0)(links.begin)
        kernel(*ins, out_ref)
        if links:
            pl.when(pl.program_id(0) == rows // ROW_TILE - 1)(links.finish)

    return host(
        body, links, [x, gain.reshape(1, dim), cos_tab, sin_tab] + weights,
        [row_block(dim), pl.BlockSpec((1, dim), lambda i: (0, 0)), row_block(HEAD_DIM), row_block(HEAD_DIM)]
        + [pl.BlockSpec(w.shape, lambda i: (0, 0), pipeline_mode=pl.Buffered(1)) for w in weights],
        jax.ShapeDtypeStruct((rows, out_cols), jnp.bfloat16), row_block(out_cols), [],
        (rows // ROW_TILE,), 2 * rows * dim * w_cols, 2 * dim * (rows + w_cols))


class Ring:
    n_remote, n_sub = 12, 2

    def __init__(self, axis, size, partial, base, base_row, gain, ring_id):
        self.axis, self.size, self.base_row, self.ring_id = axis, size, base_row, ring_id
        self.pieces, self.half, self.dim = partial.shape
        self.rows = self.half // self.n_sub
        self.normed = gain is not None
        self.operands = [partial, base] + ([gain.reshape(1, self.dim)] if self.normed else [])
        any_spec = pl.BlockSpec(memory_space=pl.ANY)
        self.in_specs = [any_spec, any_spec] + ([pl.BlockSpec(memory_space=pltpu.VMEM)] if self.normed else [])
        shapes = [(self.pieces, self.half, self.dim)] + ([(2, self.half, self.dim)] if self.normed else [])
        self.out_shape = [jax.ShapeDtypeStruct(shape, jnp.bfloat16) for shape in shapes]
        self.out_specs = [any_spec] * len(shapes)
        buf = lambda n: pltpu.VMEM((n, self.half, self.dim), jnp.bfloat16)
        sems = lambda n: pltpu.SemaphoreType.DMA((self.n_sub * n,))
        self.scratch = [buf(6), buf(6), buf(2), sems(self.n_remote), sems(self.n_remote), sems(10)]
        self.steps = [self.begin]
        for kind in (self.pass_on, self.add_up, self.relay):
            self.steps += [functools.partial(kind, sub) for sub in range(self.n_sub)]
        self.steps.append(self.finish)

    def bind(self, ins, outs, scratch):
        partial, base = ins[:2]
        gathered = outs[0]
        arrived, local, sent, self.send_sem, self.recv_sem, self.local_sem = scratch
        index = lax.axis_index(self.axis)
        fwd, back = lax.rem(index + 1, self.size), lax.rem(index + self.size - 1, self.size)
        self.neighbours = (fwd, back)
        self.arrived, self.local, self.sent = arrived, local, sent
        self.gain = ins[2] if self.normed else None
        self.remote, self.copies = [], []
        for sub in range(self.n_sub):
            part = pl.ds(sub * self.rows, self.rows)
            at = lambda ref, n: ref.at[n, part]
            self.remote.append([
                (at(partial, 6), at(arrived, 0), fwd), (at(partial, 7), at(arrived, 1), back),
                (at(partial, 5), at(arrived, 2), fwd), (at(partial, 2), at(arrived, 3), back),
                (at(local, 0), at(arrived, 4), fwd), (at(local, 1), at(arrived, 5), back),
                (at(sent, 0), at(gathered, 2), fwd), (at(sent, 1), at(gathered, 5), back),
                (at(sent, 1), at(gathered, 3), fwd), (at(sent, 0), at(gathered, 4), back),
                (at(gathered, 2), at(gathered, 6), fwd), (at(gathered, 5), at(gathered, 7), back),
            ])
            if self.base_row is None:
                rows = [at(base, 0), at(base, 1)]
            else:
                start = self.base_row + sub * self.rows + index * (2 * self.half)
                rows = [base.at[pl.ds(pl.multiple_of(start + n * self.half, self.rows), self.rows)] for n in range(2)]
            self.copies.append([
                (at(partial, 4), at(local, 0)), (at(partial, 3), at(local, 1)), (at(partial, 0), at(local, 2)), (at(partial, 1), at(local, 3)),
                (rows[0], at(local, 4)), (rows[1], at(local, 5)), (at(sent, 0), at(gathered, 0)), (at(sent, 1), at(gathered, 1)),
            ] + ([(at(local, 4), at(outs[1], 0)), (at(local, 5), at(outs[1], 1))] if self.normed else []))

    def rdma(self, sub, n):
        src, dst, peer = self.remote[sub][n]
        sem = sub * self.n_remote + n
        return pltpu.make_async_remote_copy(src_ref=src, dst_ref=dst, send_sem=self.send_sem.at[sem], recv_sem=self.recv_sem.at[sem],
                                            device_id={self.axis: peer}, device_id_type=pl.DeviceIdType.MESH)

    def copy(self, sub, n):
        src, dst = self.copies[sub][n]
        return pltpu.make_async_copy(src, dst, self.local_sem.at[sub * 10 + n])

    def begin(self):
        barrier = pltpu.get_barrier_semaphore()
        for peer in self.neighbours:
            pl.semaphore_signal(barrier, inc=1, device_id={self.axis: peer}, device_id_type=pl.DeviceIdType.MESH)
        pl.semaphore_wait(barrier, 2)
        for sub in range(self.n_sub):
            for n in range(4):
                self.rdma(sub, n).start()
        for sub in range(self.n_sub):
            for n in range(6):
                self.copy(sub, n).start()

    def pass_on(self, sub):
        part = pl.ds(sub * self.rows, self.rows)
        for n in range(2):
            self.copy(sub, n).wait()
            self.rdma(sub, n).wait_recv()
            self.local[n, part] = (self.local[n, part].astype(jnp.float32) + self.arrived[n, part].astype(jnp.float32)).astype(jnp.bfloat16)
        for n in range(2):
            self.rdma(sub, 4 + n).start()

    def add_up(self, sub):
        part = pl.ds(sub * self.rows, self.rows)
        for n in range(2, 6):
            self.copy(sub, n).wait()
            self.rdma(sub, n).wait_recv()
        for n, (a, b) in enumerate(((4, 3), (2, 5))):
            terms = (self.local[4 + n, part], self.local[2 + n, part], self.arrived[a, part], self.arrived[b, part])
            total = functools.reduce(jnp.add, [term.astype(jnp.float32) for term in terms]).astype(jnp.bfloat16)
            if self.normed:
                self.local[4 + n, part] = total
                self.sent[n, part] = rms_norm(total, self.gain[...])
            else:
                self.sent[n, part] = total
        for n in range(6, 10):
            self.rdma(sub, n).start()
        for n in range(6, len(self.copies[sub])):
            self.copy(sub, n).start()

    def relay(self, sub):
        for n in range(2):
            self.rdma(sub, 6 + n).wait_recv()
            self.rdma(sub, 10 + n).start()

    def finish(self):
        for sub in range(self.n_sub):
            for n in range(8, 12):
                self.rdma(sub, n).wait_recv()
            for n in range(12):
                self.rdma(sub, n).wait_send()
            for n in range(6, len(self.copies[sub])):
                self.copy(sub, n).wait()


class Links:
    def __init__(self, axis, size, operands, n_out, ring_id):
        self.axis, self.size, self.operands, self.ring_id = axis, size, operands, ring_id
        any_spec = pl.BlockSpec(memory_space=pl.ANY)
        self.in_specs = [any_spec] * len(operands)
        self.out_shape = [jax.ShapeDtypeStruct(operands[0].shape, jnp.bfloat16)] * n_out
        self.out_specs = [any_spec] * n_out
        self.scratch = [pltpu.SemaphoreType.DMA((5,)), pltpu.SemaphoreType.DMA((5,))]

    def bind(self, ins, outs, scratch):
        self.ins, self.outs = ins, outs
        self.send_sem, self.recv_sem = scratch
        index = lax.axis_index(self.axis)
        ahead, behind = lax.rem(index + 2, self.size), lax.rem(index + self.size - 2, self.size)
        mate = index + 1 - 2 * lax.rem(index, 2)
        self.neighbours = (ahead, behind, mate)
        if len(ins) == 1:
            self.remote = [(ins[0], outs[0], ahead), (ins[0], outs[1], behind), (ins[0], outs[2], mate)]
        else:
            middle = ins[0].shape[0] // 2
            lower, upper = pl.ds(0, middle), pl.ds(middle, middle)
            self.remote = [
                (ins[0].at[lower], outs[0].at[lower], ahead), (ins[1].at[upper], outs[0].at[upper], behind),
                (ins[0], outs[1], mate), (ins[1], outs[3], mate), (outs[0], outs[2], mate),
            ]

    def rdma(self, n):
        src, dst, peer = self.remote[n]
        return pltpu.make_async_remote_copy(src_ref=src, dst_ref=dst, send_sem=self.send_sem.at[n], recv_sem=self.recv_sem.at[n],
                                            device_id={self.axis: peer}, device_id_type=pl.DeviceIdType.MESH)

    def begin(self):
        barrier = pltpu.get_barrier_semaphore()
        for peer in self.neighbours:
            pl.semaphore_signal(barrier, inc=1, device_id={self.axis: peer}, device_id_type=pl.DeviceIdType.MESH)
        pl.semaphore_wait(barrier, len(self.neighbours))
        for n in range(min(len(self.remote), 4)):
            self.rdma(n).start()

    def finish(self):
        for n in range(len(self.remote)):
            self.rdma(n).wait_send()
            if len(self.remote) == 3:
                self.rdma(n).wait_recv()


def params(ring):
    if ring is None:
        return pltpu.CompilerParams(vmem_limit_bytes=VMEM_LIMIT)
    return pltpu.CompilerParams(vmem_limit_bytes=VMEM_LIMIT, collective_id=ring.ring_id, has_side_effects=True)


def host(kernel, ring, operands, in_specs, out_shape, out_specs, scratch, grid, flops, nbytes):
    n_in, n_ring = len(operands), len(ring.operands) if ring else 0

    def body(*refs):
        ins, rest = refs[:n_in], refs[n_in:]
        ring_ins, rest = rest[:n_ring], rest[n_ring:]
        out, rest = rest[0], rest[1:]
        if ring:
            ring_outs, rest = rest[:len(ring.out_shape)], rest[len(ring.out_shape):]
            ring.bind(ring_ins, ring_outs, rest[len(scratch):])
        kernel(ins, out, rest[:len(scratch)], ring)

    out = pl.pallas_call(
        body,
        out_shape=[out_shape] + (ring.out_shape if ring else []),
        grid=grid,
        in_specs=in_specs + (ring.in_specs if ring else []),
        out_specs=[out_specs] + (ring.out_specs if ring else []),
        scratch_shapes=scratch + (ring.scratch if ring else []),
        compiler_params=params(ring),
        cost_estimate=pl.CostEstimate(flops=flops, bytes_accessed=nbytes, transcendentals=0),
    )(*operands, *(ring.operands if ring else []))
    return out if ring else out[0]


def attention(queries, blocks, w_o, chunk, rows, kv_heads, axis, cp_size, tp_axis, tp_size, ring=None):
    q_cols = queries.shape[1] // kv_heads
    heads = q_cols // HEAD_DIM
    span = blocks[0].shape[0]
    row_start = chunk * rows
    depth, dim = w_o.shape
    piece = rows // tp_size
    half = piece // 2
    n_cols = dim // FF_TILE
    given = [n for n, block in enumerate(blocks) if block is not None]

    def kernel(ins, part_ref, scratch, ring):
        links = ring if isinstance(ring, Links) else None
        ring = None if links else ring
        q_ref, w_ref = ins[0], ins[-1]
        block_refs = dict(zip(given, ins[1:-1]))
        if links:
            block_refs.update(zip((2, 5, 6, 7), links.outs))
        k_buf, v_buf, m_ref, l_ref, acc_ref, sems, turned, w_buf, part_buf, w_sem, part_sem = scratch
        kv_head = pl.program_id(0)
        index = lax.axis_index(axis)
        odd = lax.rem(index, 2)
        if ring or links:
            pl.when(kv_head == 0)((ring or links).begin)
        slots = [0, 2, 4, 6] + [jnp.where(odd == 1, a, b) for a, b in ((1, 7), (3, 1), (5, 3), (7, 5))]
        copies = []
        for n, slot in enumerate(slots):
            start = slot * span if n < 4 else pl.multiple_of(slot * span, span)
            for part, buf in enumerate((k_buf, v_buf)):
                col = pl.multiple_of((part * kv_heads + kv_head) * HEAD_DIM, HEAD_DIM)
                copies.append(pltpu.make_async_copy(block_refs[n].at[:, pl.ds(col, HEAD_DIM)], buf.at[pl.ds(start, span)], sems.at[2 * n + part]))
        late = [2 * n + part for n in (2, 5, 6, 7) for part in range(2)] if links else []
        early = [n for n in range(2, 16) if n not in late]

        def start_late():
            for n in late:
                copies[n].start()

        def wait_late():
            for n in late:
                copies[n].wait()

        def take(arrivals, block_ids):
            for n in arrivals:
                links.rdma(n).wait_recv()
            for n in block_ids:
                for part in range(2):
                    copies[2 * n + part].start()

        def settle(block_ids):
            for n in block_ids:
                for part in range(2):
                    copies[2 * n + part].wait()

        for n in [0, 1] + early:
            copies[n].start()
        if links:
            pl.when(kv_head > 0)(start_late)
        w_copy = pltpu.make_async_copy(w_ref, w_buf, w_sem)
        pl.when(kv_head == 0)(w_copy.start)

        def tile_step(start, masked):
            k_tile = k_buf[pl.ds(start, KEY_TILE)]
            v_tile = v_buf[pl.ds(start, KEY_TILE)]
            for head in range(heads):
                scores = lax.dot_general(q_ref[:, head * HEAD_DIM:(head + 1) * HEAD_DIM], k_tile, (((1,), (1,)), ((), ())), preferred_element_type=jnp.float32)
                if masked:
                    q_pos = row_start + lax.broadcasted_iota(jnp.int32, scores.shape, 0)
                    k_pos = start + lax.broadcasted_iota(jnp.int32, scores.shape, 1)
                    scores = jnp.where(k_pos <= q_pos, scores, MASK_VALUE)
                parts = [scores[:, n:n + 128] for n in range(0, KEY_TILE, 128)]
                new_max = jnp.broadcast_to(jnp.max(functools.reduce(jnp.maximum, parts), axis=1, keepdims=True), (rows, 128))
                if not masked:
                    old_max = m_ref[head]
                    new_max = jnp.maximum(old_max, new_max)
                probs = [jnp.exp2((part - new_max) * SCORE_EXP2) for part in parts]
                tile_sum = functools.reduce(jnp.add, probs)
                weighted = jnp.dot(jnp.concatenate(probs, axis=1).astype(jnp.bfloat16), v_tile, preferred_element_type=jnp.float32)
                if masked:
                    l_ref[head] = tile_sum
                    acc_ref[head] = weighted
                else:
                    rescale = jnp.exp2((old_max - new_max) * SCORE_EXP2)
                    l_ref[head] = l_ref[head] * rescale + tile_sum
                    acc_ref[head] = acc_ref[head] * rescale + weighted
                m_ref[head] = new_max

        for copy in copies[:2]:
            copy.wait()
        own_full = row_start // KEY_TILE
        tile_step(own_full * KEY_TILE, True)
        for n in early:
            copies[n].wait()
        if links:
            pl.when(kv_head > 0)(wait_late)
        per_block = span // KEY_TILE
        n_full = own_full + index * per_block
        trips = 7 * per_block if links else jnp.maximum(n_full, 1) if ring else n_full
        last = kv_heads - 1

        def full_step(i, carry):
            if ring:
                for step, (head_step, at) in enumerate(((0, 2), (0, 5), (last, 0), (last, 2), (last, 4))):
                    pl.when((kv_head == head_step) & (i == trips * at // 7))(ring.steps[1 + step])

            @pl.when(i < n_full)
            def _():
                tile = jnp.where(i < own_full, i, i - own_full + per_block)
                tile_step(pl.multiple_of(tile * KEY_TILE, KEY_TILE), False)
            return carry

        def arrival_step(i, carry):
            place = i // per_block

            def far_here():
                take((0, 1), (2,))
                links.rdma(4).start()
                settle((2,))

            def mates_here():
                take((2, 3), (5, 7))
                settle((5, 7))

            def far_mate_here():
                take((4,), (6,))
                settle((6,))

            for at, action in ((3, mates_here), (4, far_here), (6, far_mate_here)):
                pl.when((kv_head == 0) & (i == at * per_block))(action)
            slot = jnp.int32(0)
            for n, (a, b) in enumerate(((2, 2), (6, 6), (1, 7), (3, 1), (7, 5), (4, 4), (5, 3))):
                slot = jnp.where(place == n, jnp.where(odd == 1, a, b), slot)

            @pl.when(slot <= index)
            def _():
                tile_step(pl.multiple_of(slot * span + lax.rem(i, per_block) * KEY_TILE, KEY_TILE), False)
            return carry

        lax.fori_loop(0, trips, arrival_step if links else full_step, 0)
        tp_index = lax.axis_index(tp_axis)
        for place, step in enumerate((0, tp_size - 1, 1, 2)):
            from_rows = pl.ds(pl.multiple_of(lax.rem(tp_index + step, tp_size) * piece, piece), piece)
            for head in range(heads):
                col = pl.multiple_of((kv_head * heads + head) * HEAD_DIM, HEAD_DIM)
                total = jnp.sum(l_ref[head, from_rows, :], axis=1, keepdims=True)
                turned[place * piece:(place + 1) * piece, pl.ds(col, HEAD_DIM)] = (acc_ref[head, from_rows, :] / total).astype(jnp.bfloat16)

        @pl.when(kv_head == last)
        def _():
            if ring:
                ring.steps[6]()
            w_copy.wait()

            def part_copy(i):
                cols = pl.ds(pl.multiple_of(i * FF_TILE, FF_TILE), FF_TILE)
                return pltpu.make_async_copy(part_buf.at[:, :, cols], part_ref.at[:, :, cols], part_sem.at[i])

            def project_cols(i, carry):
                cols = pl.ds(pl.multiple_of(i * FF_TILE, FF_TILE), FF_TILE)
                product = jnp.dot(turned[...], w_buf[:, cols], preferred_element_type=jnp.float32)
                for n in range(2 * tp_size):
                    part_buf[n, :, cols] = product[n * half:(n + 1) * half].astype(jnp.bfloat16)
                part_copy(i).start()
                return carry

            lax.fori_loop(0, n_cols, project_cols, 0)
            for i in range(n_cols):
                part_copy(i).wait()
            if ring or links:
                (ring or links).finish()

    return host(
        kernel, ring, [queries] + [blocks[n] for n in given] + [w_o],
        [pl.BlockSpec((rows, q_cols), lambda i: (chunk, i))] + [pl.BlockSpec(memory_space=pl.ANY)] * (len(given) + 1),
        jax.ShapeDtypeStruct((2 * tp_size, half, dim), jnp.bfloat16), pl.BlockSpec(memory_space=pl.ANY),
        [
            pltpu.VMEM((cp_size * span, HEAD_DIM), jnp.bfloat16),
            pltpu.VMEM((cp_size * span, HEAD_DIM), jnp.bfloat16),
            pltpu.VMEM((heads, rows, 128), jnp.float32),
            pltpu.VMEM((heads, rows, 128), jnp.float32),
            pltpu.VMEM((heads, rows, HEAD_DIM), jnp.float32),
            pltpu.SemaphoreType.DMA((16,)),
            pltpu.VMEM((rows, depth), jnp.bfloat16),
            pltpu.VMEM((depth, dim), jnp.bfloat16),
            pltpu.VMEM((2 * tp_size, half, dim), jnp.bfloat16),
            pltpu.SemaphoreType.DMA,
            pltpu.SemaphoreType.DMA((n_cols,)),
        ],
        (kv_heads,), 4 * rows * q_cols * kv_heads * span * cp_size + 2 * rows * depth * dim,
        4 * kv_heads * cp_size * span * HEAD_DIM + 2 * depth * dim)


def store_pieces(value, ref):
    pieces, half, unused = ref.shape
    for n in range(pieces):
        ref[n] = value[n * half:(n + 1) * half].astype(jnp.bfloat16)


def mlp(pieces, w_gate, w_up, w_down, tile, ring):
    n_pieces, half, dim = pieces.shape
    rows = n_pieces * half
    width = w_gate.shape[1]
    n_up, n_down = width // tile, dim // tile

    def kernel(ins, out_ref, scratch, ring):
        (pieces_ref, gate_ref, up_ref, down_ref), (act, normed_ref, row_sem) = ins, scratch
        g = pl.program_id(0)
        for step, at in enumerate((0, 2, 4, 6, 8, 9, 12)):
            pl.when(g == at)(ring.steps[step])

        @pl.when(g == 0)
        def _():
            rows_copy = pltpu.make_async_copy(pieces_ref, normed_ref, row_sem)
            rows_copy.start()
            rows_copy.wait()

        @pl.when(g < n_up)
        def _():
            gate = jnp.dot(normed_ref[...], gate_ref[...], preferred_element_type=jnp.float32)
            up = jnp.dot(normed_ref[...], up_ref[...], preferred_element_type=jnp.float32)
            act[:, pl.ds(pl.multiple_of(g * tile, tile), tile)] = (jax.nn.silu(gate) * up).astype(jnp.bfloat16)

        @pl.when(g >= n_up)
        def _():
            store_pieces(jnp.dot(act[...], down_ref[...], preferred_element_type=jnp.float32), out_ref)

        pl.when(g == n_up + n_down - 1)(ring.finish)

    up_spec = pl.BlockSpec((dim, tile), lambda i: (0, jnp.minimum(i, n_up - 1)))
    return host(
        kernel, ring, [pieces.reshape(rows, dim), w_gate, w_up, w_down],
        [pl.BlockSpec(memory_space=pl.ANY), up_spec, up_spec,
         pl.BlockSpec((width, tile), lambda i: (0, jnp.maximum(i - n_up, 0)))],
        jax.ShapeDtypeStruct((n_pieces, half, dim), jnp.bfloat16), pl.BlockSpec((n_pieces, half, tile), lambda i: (0, 0, jnp.maximum(i - n_up, 0))),
        [pltpu.VMEM((rows, width), jnp.bfloat16), pltpu.VMEM((rows, dim), jnp.bfloat16), pltpu.SemaphoreType.DMA], (n_up + n_down,), 6 * rows * dim * width, 6 * dim * width + 6 * rows * dim)


def all_reduce(ring):
    def body(*refs):
        n_in, n_out = len(ring.operands), len(ring.out_shape)
        ring.bind(refs[:n_in], refs[n_in:n_in + n_out], refs[n_in + n_out:])
        for step in (0, 1, 2, 3, 4, 5, 6, 7):
            ring.steps[step]()

    return pl.pallas_call(body, out_shape=ring.out_shape, in_specs=ring.in_specs, out_specs=ring.out_specs, scratch_shapes=ring.scratch,
                          compiler_params=params(ring))(*ring.operands)


def assemble(chunks, axis, size):
    n_pieces, half, dim = chunks[0].shape
    total = len(chunks) * n_pieces

    def kernel(*refs):
        ins, (out_ref, buf, in_sem, out_sem) = refs[:len(chunks)], refs[len(chunks):]
        index = lax.axis_index(axis)
        places = []
        for n in range(total):
            step = (0, size - 1, 1, 2)[n % n_pieces // 2]
            start = (n // n_pieces * n_pieces + n % 2 + 2 * lax.rem(index + step, size)) * half
            places.append(pl.ds(pl.multiple_of(start, half), half))
        loads = [pltpu.make_async_copy(ins[n // n_pieces].at[n % n_pieces], buf.at[n], in_sem.at[n]) for n in range(total)]
        stores = [pltpu.make_async_copy(buf.at[n], out_ref.at[places[n]], out_sem.at[n]) for n in range(total)]
        for load in loads:
            load.start()
        for load, store in zip(loads, stores):
            load.wait()
            store.start()
        for store in stores:
            store.wait()

    return pl.pallas_call(
        kernel,
        out_shape=jax.ShapeDtypeStruct((total * half, dim), jnp.bfloat16),
        in_specs=[pl.BlockSpec(memory_space=pl.ANY)] * len(chunks),
        out_specs=pl.BlockSpec(memory_space=pl.ANY),
        scratch_shapes=[pltpu.VMEM((total, half, dim), jnp.bfloat16), pltpu.SemaphoreType.DMA((total,)), pltpu.SemaphoreType.DMA((total,))],
        compiler_params=pltpu.CompilerParams(vmem_limit_bytes=VMEM_LIMIT),
        cost_estimate=pl.CostEstimate(flops=0, bytes_accessed=4 * total * half * dim, transcendentals=0),
    )(*chunks)


def solution(mesh):
    cp_size = mesh.shape['cp']
    tp_size = mesh.shape['tp']
    row_spec = P(('dp', 'cp'), None)
    cache_spec = P(('dp', 'cp'), 'tp', None)
    col_spec = P(None, 'tp')
    split_rows = P('tp', None)
    vec_spec = P(None)

    def local_layer(x, attn_gain, w_q, w_k, w_v, w_o, mlp_gain, w_gate, w_up, w_down):
        tok_dev = x.shape[0]
        kv_local = w_k.shape[1] // HEAD_DIM
        kv_cols = w_k.shape[1]
        cp_index = lax.axis_index('cp')
        cos_tab, sin_tab = rope_tables(cp_index * tok_dev + jnp.arange(tok_dev))
        own = project(kv_kernel, x, attn_gain, cos_tab, sin_tab, [w_k, w_v], 2 * kv_cols)
        queries, low, high, mate = project(q_kernel, x, attn_gain, cos_tab, sin_tab, [w_q], w_q.shape[1], Links('cp', cp_size, [own], 3, 4))
        blocks = [own, low, None, high, mate, None, None, None]
        rows = tok_dev // 2

        def attend(chunk, ring=None):
            return attention(queries, blocks, w_o, chunk, rows, kv_local, 'cp', cp_size, 'tp', tp_size, ring)

        def reduce_over_tp(partial, base, base_row, gain, ring_id):
            return Ring('tp', tp_size, partial, base, base_row, gain, ring_id)

        part0, far, mate_low, mate_far, mate_high = attend(0, Links('cp', cp_size, [low, high], 4, 5))
        blocks = [own, low, far, high, mate, mate_low, mate_far, mate_high]
        part1, normed0, hidden0 = attend(1, reduce_over_tp(part0, x, 0, mlp_gain, 0))
        down0, normed1, hidden1 = mlp(normed0, w_gate, w_up, w_down, FF_TILE, reduce_over_tp(part1, x, rows, mlp_gain, 1))
        down1, out0 = mlp(normed1, w_gate, w_up, w_down, FF_TILE, reduce_over_tp(down0, hidden0, None, None, 2))
        out1 = all_reduce(reduce_over_tp(down1, hidden1, None, None, 3))[0]
        x_out = assemble([out0, out1], 'tp', tp_size)
        cache_shape = (tok_dev, kv_local, HEAD_DIM)
        return x_out, own[:, :kv_cols].reshape(cache_shape), own[:, kv_cols:].reshape(cache_shape)

    return jax.shard_map(local_layer, mesh=mesh,
                         in_specs=(row_spec, vec_spec, col_spec, col_spec, col_spec, split_rows, vec_spec, col_spec, col_spec, split_rows),
                         out_specs=(row_spec, cache_spec, cache_spec), check_vma=False)
```

profile of v0, /device:TPU:102, one launch (start us, length us, event | category | flops | bytes accessed | tf_op | source)
XLA Modules:
  0.0 414.6 jit_solution(11317225448076502045)
XLA Ops:
  0.6 0.0 copy-start.1
  0.7 1.9 fusion
  2.6 1.3 pad_maximum_fusion
  3.9 0.0 copy-done.1
  3.9 0.6 reshape.38.refs_1_
  4.5 10.9 %shard_map.121.refs_5_.refs_1_ = bf16[1024,512]{1,0:T(8,128)(2,1)} custom-call(bf16[1024,4096]{1,0:T(8,128)(2,1)} %refs_5_.5, bf16[1,4096]{1,0:T(2,128)(2,1)} %reshape.38.refs_1_, f32[1024,128]{1,0:T(8,128)} %get-tuple-element.42.refs_2_, f32[1024,128]{1,0:T(8,128)} %get-tuple-element.43.refs_3_, bf16[4096,256]{1,0:T(8,128)(2,1)} %refs_4_.2, ...), custom_call_target="tpu_custom_call" | custom-call | flops 4294967296 | bytes 12582912 | tf_op jit(solution)/shard_map/pallas_call | solution.py:259
  15.4 31.3 %shard_map.122 = (bf16[1024,1024]{1,0:T(8,128)(2,1)}, bf16[1024,512]{1,0:T(8,128)(2,1)}, bf16[1024,512]{1,0:T(8,128)(2,1)}, bf16[1024,512]{1,0:T(8,128)(2,1)}) custom-call(bf16[1024,4096]{1,0:T(8,128)(2,1)} %refs_5_.5, bf16[1,4096]{1,0:T(2,128)(2,1)} %reshape.38.refs_1_, f32[1024,128]{1,0:T(8,128)} %get-tuple-element.42.refs_2_, ...), custom_call_target="tpu_custom_call" | custom-call | flops 8589934592 | bytes 16777216 | tf_op jit(solution)/shard_map/pallas_call | solution.py:259
  46.7 0.0 copy-start.2
  46.7 57.8 %shard_map.123 = (bf16[8,64,4096]{2,1,0:T(8,128)(2,1)}, bf16[1024,512]{1,0:T(8,128)(2,1)}, bf16[1024,512]{1,0:T(8,128)(2,1)}, bf16[1024,512]{1,0:T(8,128)(2,1)}, bf16[1024,512]{1,0:T(8,128)(2,1)}) custom-call(bf16[1024,1024]{1,0:T(8,128)(2,1)} %get-tuple-element.20.refs_0_, bf16[1024,512]{1,0:T(8,128)(2,1)} %shard_map.121.refs_5_.refs_1_, ...), custom_call_target="tpu_custom_call" | custom-call | flops 21474836480 | bytes 16777216 | tf_op jit(solution)/shard_map/pallas_call | solution.py:259
  104.5 0.0 copy-done.2
  104.6 0.6 reshape.39.refs_12_.refs_6_
  105.2 71.5 %shard_map.124 = (bf16[8,64,4096]{2,1,0:T(8,128)(2,1)}, bf16[8,64,4096]{2,1,0:T(8,128)(2,1)}, bf16[2,64,4096]{2,1,0:T(8,128)(2,1)}) custom-call(bf16[1024,1024]{1,0:T(8,128)(2,1)} %get-tuple-element.20.refs_0_, bf16[1024,512]{1,0:T(8,128)(2,1)} %shard_map.121.refs_5_.refs_1_, bf16[1024,512]{1,0:T(8,128)(2,1)} %get-tuple-element.21.refs_2_.refs_6_, ...), custom_call_target="tpu_custom_call" | custom-call | flops 21474836480 | bytes 16777216 | tf_op jit(solution)/shard_map/pallas_call | solution.py:259
  176.7 79.2 %shard_map.125 = (bf16[8,64,4096]{2,1,0:T(8,128)(2,1)}, bf16[8,64,4096]{2,1,0:T(8,128)(2,1)}, bf16[2,64,4096]{2,1,0:T(8,128)(2,1)}) custom-call(bf16[512,4096]{1,0:T(8,128)(2,1)} %bitcast.2, bf16[4096,3584]{1,0:T(8,128)(2,1)} %refs_1_.3, bf16[4096,3584]{1,0:T(8,128)(2,1)} %refs_2_.3, bf16[3584,4096]{1,0:T(8,128)(2,1)} %refs_3_.3, ...), custom_call_target="tpu_custom_call" | custom-call | flops 45097156608 | bytes 100663296 | tf_op jit(solution)/shard_map/pallas_call | solution.py:259
  255.9 77.7 %shard_map.126 = (bf16[8,64,4096]{2,1,0:T(8,128)(2,1)}, bf16[8,64,4096]{2,1,0:T(8,128)(2,1)}) custom-call(bf16[512,4096]{1,0:T(8,128)(2,1)} %bitcast.3, bf16[4096,3584]{1,0:T(8,128)(2,1)} %refs_1_.3, bf16[4096,3584]{1,0:T(8,128)(2,1)} %refs_2_.3, bf16[3584,4096]{1,0:T(8,128)(2,1)} %refs_3_.3, bf16[8,64,4096]{2,1,0:T(8,128)(2,1)} %get-tuple-element.32.refs_4_, ...), custom_call_target="tpu_custom_call" | custom-call | flops 45097156608 | bytes 100663296 | tf_op jit(solution)/shard_map/pallas_call | solution.py:259
  333.6 72.4 %shard_map.127.refs_1_ = bf16[8,64,4096]{2,1,0:T(8,128)(2,1)} custom-call(bf16[8,64,4096]{2,1,0:T(8,128)(2,1)} %get-tuple-element.35.refs_0_, bf16[2,64,4096]{2,1,0:T(8,128)(2,1)} %get-tuple-element.36.refs_1_), custom_call_target="tpu_custom_call" | custom-call | tf_op jit(solution)/shard_map/pallas_call | solution.py:516
  406.0 0.0 copy-start
  406.0 6.7 %shard_map.128 = bf16[1024,4096]{1,0:T(8,128)(2,1)} custom-call(bf16[8,64,4096]{2,1,0:T(8,128)(2,1)} %get-tuple-element.34.refs_0_, bf16[8,64,4096]{2,1,0:T(8,128)(2,1)} %shard_map.127.refs_1_), custom_call_target="tpu_custom_call" | custom-call | bytes 16777216 | tf_op jit(solution)/shard_map/pallas_call | solution.py:542
  412.6 0.0 copy-done
  412.6 0.1 fusion.1
  412.7 0.9 reshape.42
  413.6 0.9 reshape.43
  (2 shorter events, 0.0 us)
Async XLA Ops:
  0.6 3.3 copy-start.1
  46.7 57.9 %copy-start.2 = (bf16[4096]{0:T(1024)(128)(2,1)S(1)}, bf16[4096]{0:T(1024)(128)(2,1)}, u32[]{:S(2)}) copy-start(bf16[4096]{0:T(1024)(128)(2,1)} %param.16) | copy-start | bytes 24580
  406.0 6.7 %copy-start = (bf16[1024,512]{1,0:T(8,128)(2,1)S(1)}, bf16[1024,512]{1,0:T(8,128)(2,1)}, u32[]{:S(2)}) copy-start(bf16[1024,512]{1,0:T(8,128)(2,1)} %shard_map.121.refs_5_.refs_1_) | copy-start | bytes 3145732
where the time goes:
time: 415 us
  Pallas kernels  407 us (98%)
    pallas_call x6, Pallas kernels, host(): pl.pallas_call(body, out_shape=[out_shape] + (ring.out_shape if ring else...  328 us
    pallas_call x1, Pallas kernels, all_reduce(): pl.pallas_call(body, out_shape=ring.out_shape, in_specs=ring.in_specs, ou...  72.4 us

commit v1 on v0

--- a/solution.py
+++ b/solution.py
@@ -37,42 +37,58 @@
     return (wide * cos_t + pltpu.roll(wide, HEAD_DIM // 2, 1) * sin_t).astype(jnp.bfloat16)
 
 
-def kv_kernel(x_ref, gain_ref, cos_ref, sin_ref, w_k_ref, w_v_ref, kv_ref):
-    normed = rms_norm(x_ref[...], gain_ref[...])
-    width = w_k_ref.shape[1]
-    keys = jnp.dot(normed, w_k_ref[...], preferred_element_type=jnp.float32)
-    for head in range(width // HEAD_DIM):
-        cols = slice(head * HEAD_DIM, (head + 1) * HEAD_DIM)
-        kv_ref[:, cols] = rope_head(keys[:, cols], cos_ref[...], sin_ref[...])
-    kv_ref[:, width:] = jnp.dot(normed, w_v_ref[...], preferred_element_type=jnp.float32).astype(jnp.bfloat16)
-
-
-def q_kernel(x_ref, gain_ref, cos_ref, sin_ref, w_q_ref, q_ref):
-    normed = rms_norm(x_ref[...], gain_ref[...])
-    queries = jnp.dot(normed, w_q_ref[...], preferred_element_type=jnp.float32)
-    for head in range(w_q_ref.shape[1] // HEAD_DIM):
-        cols = slice(head * HEAD_DIM, (head + 1) * HEAD_DIM)
-        q_ref[:, cols] = rope_head(queries[:, cols], cos_ref[...], sin_ref[...])
-
-
-def project(kernel, x, gain, cos_tab, sin_tab, weights, out_cols, links=None):
+def project(x, gain, cos_tab, sin_tab, w_k, w_v, w_q, links):
     rows, dim = x.shape
-    row_block = lambda cols: pl.BlockSpec((ROW_TILE, cols), lambda i: (i, 0))
-    w_cols = sum(w.shape[1] for w in weights)
-
-    def body(ins, out_ref, scratch, links):
-        if links:
-            pl.when(pl.program_id(0) == 0)(links.begin)
-        kernel(*ins, out_ref)
-        if links:
-            pl.when(pl.program_id(0) == rows // ROW_TILE - 1)(links.finish)
-
+    width, q_cols = w_k.shape[1], w_q.shape[1]
+    n_tiles = rows // ROW_TILE
+
+    def kernel(ins, q_ref, scratch, links):
+        (x_ref, gain_ref, cos_ref, sin_ref, w_k_ref, w_v_ref, w_q_ref), (own,) = ins, scratch
+        g = pl.program_id(0)
+        kv_out = links.outs[3]
+        links.source(own, ROW_TILE)
+        pl.when(g == 0)(links.begin)
+
+        def send(tile):
+            for n in range(3):
+                links.rdma(3 * tile + n).start()
+
+        for tile in range(n_tiles):
+            pl.when(g == tile + 1)(functools.partial(send, tile))
+        store = pltpu.make_async_copy(own, kv_out, links.local_sem)
+        pl.when(g == n_tiles)(store.start)
+        normed = rms_norm(x_ref[...], gain_ref[...])
+
+        @pl.when(g < n_tiles)
+        def _():
+            tile = pl.ds(pl.multiple_of(g * ROW_TILE, ROW_TILE), ROW_TILE)
+            keys = jnp.dot(normed, w_k_ref[...], preferred_element_type=jnp.float32)
+            for head in range(width // HEAD_DIM):
+                cols = slice(head * HEAD_DIM, (head + 1) * HEAD_DIM)
+                own[tile, cols] = rope_head(keys[:, cols], cos_ref[...], sin_ref[...])
+            own[tile, width:] = jnp.dot(normed, w_v_ref[...], preferred_element_type=jnp.float32).astype(jnp.bfloat16)
+
+        @pl.when(g >= n_tiles)
+        def _():
+            queries = jnp.dot(normed, w_q_ref[...], preferred_element_type=jnp.float32)
+            for head in range(q_cols // HEAD_DIM):
+                cols = slice(head * HEAD_DIM, (head + 1) * HEAD_DIM)
+                q_ref[:, cols] = rope_head(queries[:, cols], cos_ref[...], sin_ref[...])
+
+        @pl.when(g == 2 * n_tiles - 1)
+        def _():
+            links.finish()
+            store.wait()
+
+    row_block = lambda cols: pl.BlockSpec((ROW_TILE, cols), lambda i: (lax.rem(i, n_tiles), 0))
+    weights = [w_k, w_v, w_q]
     return host(
-        body, links, [x, gain.reshape(1, dim), cos_tab, sin_tab] + weights,
+        kernel, links, [x, gain.reshape(1, dim), cos_tab, sin_tab] + weights,
         [row_block(dim), pl.BlockSpec((1, dim), lambda i: (0, 0)), row_block(HEAD_DIM), row_block(HEAD_DIM)]
         + [pl.BlockSpec(w.shape, lambda i: (0, 0), pipeline_mode=pl.Buffered(1)) for w in weights],
-        jax.ShapeDtypeStruct((rows, out_cols), jnp.bfloat16), row_block(out_cols), [],
-        (rows // ROW_TILE,), 2 * rows * dim * w_cols, 2 * dim * (rows + w_cols))
+        jax.ShapeDtypeStruct((rows, q_cols), jnp.bfloat16), pl.BlockSpec((ROW_TILE, q_cols), lambda i: (jnp.maximum(i - n_tiles, 0), 0)),
+        [pltpu.VMEM((rows, 2 * width), jnp.bfloat16)],
+        (2 * n_tiles,), 2 * rows * dim * (2 * width + q_cols), 2 * dim * (2 * rows + 2 * width + q_cols))
 
 
 class Ring:
@@ -193,24 +209,22 @@
 
 
 class Links:
-    def __init__(self, axis, size, operands, n_out, ring_id):
+    def __init__(self, axis, size, operands, block, n_out, ring_id):
         self.axis, self.size, self.operands, self.ring_id = axis, size, operands, ring_id
         any_spec = pl.BlockSpec(memory_space=pl.ANY)
         self.in_specs = [any_spec] * len(operands)
-        self.out_shape = [jax.ShapeDtypeStruct(operands[0].shape, jnp.bfloat16)] * n_out
+        self.out_shape = [jax.ShapeDtypeStruct(block, jnp.bfloat16)] * n_out
         self.out_specs = [any_spec] * n_out
-        self.scratch = [pltpu.SemaphoreType.DMA((5,)), pltpu.SemaphoreType.DMA((5,))]
+        self.scratch = [pltpu.SemaphoreType.DMA((12,)), pltpu.SemaphoreType.DMA((12,)), pltpu.SemaphoreType.DMA]
 
     def bind(self, ins, outs, scratch):
         self.ins, self.outs = ins, outs
-        self.send_sem, self.recv_sem = scratch
+        self.send_sem, self.recv_sem, self.local_sem = scratch
         index = lax.axis_index(self.axis)
         ahead, behind = lax.rem(index + 2, self.size), lax.rem(index + self.size - 2, self.size)
         mate = index + 1 - 2 * lax.rem(index, 2)
         self.neighbours = (ahead, behind, mate)
-        if len(ins) == 1:
-            self.remote = [(ins[0], outs[0], ahead), (ins[0], outs[1], behind), (ins[0], outs[2], mate)]
-        else:
+        if ins:
             middle = ins[0].shape[0] // 2
             lower, upper = pl.ds(0, middle), pl.ds(middle, middle)
             self.remote = [
@@ -228,13 +242,18 @@
         for peer in self.neighbours:
             pl.semaphore_signal(barrier, inc=1, device_id={self.axis: peer}, device_id_type=pl.DeviceIdType.MESH)
         pl.semaphore_wait(barrier, len(self.neighbours))
-        for n in range(min(len(self.remote), 4)):
-            self.rdma(n).start()
+        if self.ins:
+            for n in range(4):
+                self.rdma(n).start()
+
+    def source(self, own, tile_rows):
+        self.remote = [(own.at[pl.ds(n, tile_rows)], out.at[pl.ds(n, tile_rows)], peer)
+                       for n in range(0, own.shape[0], tile_rows) for out, peer in zip(self.outs, self.neighbours)]
 
     def finish(self):
         for n in range(len(self.remote)):
             self.rdma(n).wait_send()
-            if len(self.remote) == 3:
+            if not self.ins:
                 self.rdma(n).wait_recv()
 
 
@@ -565,8 +584,8 @@
         kv_cols = w_k.shape[1]
         cp_index = lax.axis_index('cp')
         cos_tab, sin_tab = rope_tables(cp_index * tok_dev + jnp.arange(tok_dev))
-        own = project(kv_kernel, x, attn_gain, cos_tab, sin_tab, [w_k, w_v], 2 * kv_cols)
-        queries, low, high, mate = project(q_kernel, x, attn_gain, cos_tab, sin_tab, [w_q], w_q.shape[1], Links('cp', cp_size, [own], 3, 4))
+        block = (tok_dev, 2 * kv_cols)
+        queries, low, high, mate, own = project(x, attn_gain, cos_tab, sin_tab, w_k, w_v, w_q, Links('cp', cp_size, [], block, 4, 4))
         blocks = [own, low, None, high, mate, None, None, None]
         rows = tok_dev // 2
 
@@ -576,7 +595,7 @@
         def reduce_over_tp(partial, base, base_row, gain, ring_id):
             return Ring('tp', tp_size, partial, base, base_row, gain, ring_id)
 
-        part0, far, mate_low, mate_far, mate_high = attend(0, Links('cp', cp_size, [low, high], 4, 5))
+        part0, far, mate_low, mate_far, mate_high = attend(0, Links('cp', cp_size, [low, high], block, 4, 5))
         blocks = [own, low, far, high, mate, mate_low, mate_far, mate_high]
         part1, normed0, hidden0 = attend(1, reduce_over_tp(part0, x, 0, mlp_gain, 0))
         down0, normed1, hidden1 = mlp(normed0, w_gate, w_up, w_down, FF_TILE, reduce_over_tp(part1, x, rows, mlp_gain, 1))

time: 415 us -> 408 us (0.983)
  Pallas kernels: 407 us -> 401 us
    pallas_call x6 -> x5, Pallas kernels: 328 us -> 322 us  [host(): pl.pallas_call(body, out_shape=[out_shape] + (ring.out_shape if ring else...]
where the time goes in v1:
time: 408 us
  Pallas kernels  401 us (98%)
    pallas_call x5, Pallas kernels, host(): pl.pallas_call(body, out_shape=[out_shape] + (ring.out_shape if ring else...  322 us
    pallas_call x1, Pallas kernels, all_reduce(): pl.pallas_call(body, out_shape=ring.out_shape, in_specs=ring.in_specs, ou...  72.4 us

profile of v1, /device:TPU:102, one launch (start us, length us, event | category | flops | bytes accessed | tf_op | source)
XLA Modules:
  0.0 407.7 jit_solution(9526978463054294905)
XLA Ops:
  0.6 0.0 copy-start.1
  0.7 1.9 fusion
  2.6 1.3 pad_maximum_fusion
  3.9 0.0 copy-done.1
  3.9 0.6 reshape.37.refs_1_
  4.5 35.2 %shard_map.121 = (bf16[1024,1024]{1,0:T(8,128)(2,1)}, bf16[1024,512]{1,0:T(8,128)(2,1)}, bf16[1024,512]{1,0:T(8,128)(2,1)}, bf16[1024,512]{1,0:T(8,128)(2,1)}, bf16[1024,512]{1,0:T(8,128)(2,1)}) custom-call(bf16[1024,4096]{1,0:T(8,128)(2,1)} %refs_5_.5, bf16[1,4096]{1,0:T(2,128)(2,1)} %reshape.37.refs_1_, f32[1024,128]{1,0:T(8,128)} %get-tuple-element.44.refs_2_, ...), custom_call_target="tpu_custom_call" | custom-call | flops 12884901888 | bytes 29360128 | tf_op jit(solution)/shard_map/pallas_call | solution.py:278
  39.8 0.0 copy-start.2
  39.8 58.0 %shard_map.122 = (bf16[8,64,4096]{2,1,0:T(8,128)(2,1)}, bf16[1024,512]{1,0:T(8,128)(2,1)}, bf16[1024,512]{1,0:T(8,128)(2,1)}, bf16[1024,512]{1,0:T(8,128)(2,1)}, bf16[1024,512]{1,0:T(8,128)(2,1)}) custom-call(bf16[1024,1024]{1,0:T(8,128)(2,1)} %get-tuple-element.21.refs_0_, bf16[1024,512]{1,0:T(8,128)(2,1)} %get-tuple-element.22.refs_1_, ...), custom_call_target="tpu_custom_call" | custom-call | flops 21474836480 | bytes 16777216 | tf_op jit(solution)/shard_map/pallas_call | solution.py:278
  97.7 0.0 copy-done.2
  97.7 0.6 reshape.38.refs_12_.refs_6_
  98.4 71.5 %shard_map.123 = (bf16[8,64,4096]{2,1,0:T(8,128)(2,1)}, bf16[8,64,4096]{2,1,0:T(8,128)(2,1)}, bf16[2,64,4096]{2,1,0:T(8,128)(2,1)}) custom-call(bf16[1024,1024]{1,0:T(8,128)(2,1)} %get-tuple-element.21.refs_0_, bf16[1024,512]{1,0:T(8,128)(2,1)} %get-tuple-element.22.refs_1_, bf16[1024,512]{1,0:T(8,128)(2,1)} %get-tuple-element.23.refs_2_.refs_6_, ...), custom_call_target="tpu_custom_call" | custom-call | flops 21474836480 | bytes 16777216 | tf_op jit(solution)/shard_map/pallas_call | solution.py:278
  169.8 79.2 %shard_map.124 = (bf16[8,64,4096]{2,1,0:T(8,128)(2,1)}, bf16[8,64,4096]{2,1,0:T(8,128)(2,1)}, bf16[2,64,4096]{2,1,0:T(8,128)(2,1)}) custom-call(bf16[512,4096]{1,0:T(8,128)(2,1)} %bitcast.2, bf16[4096,3584]{1,0:T(8,128)(2,1)} %refs_1_.3, bf16[4096,3584]{1,0:T(8,128)(2,1)} %refs_2_.3, bf16[3584,4096]{1,0:T(8,128)(2,1)} %refs_3_.3, ...), custom_call_target="tpu_custom_call" | custom-call | flops 45097156608 | bytes 100663296 | tf_op jit(solution)/shard_map/pallas_call | solution.py:278
  249.1 77.7 %shard_map.125 = (bf16[8,64,4096]{2,1,0:T(8,128)(2,1)}, bf16[8,64,4096]{2,1,0:T(8,128)(2,1)}) custom-call(bf16[512,4096]{1,0:T(8,128)(2,1)} %bitcast.3, bf16[4096,3584]{1,0:T(8,128)(2,1)} %refs_1_.3, bf16[4096,3584]{1,0:T(8,128)(2,1)} %refs_2_.3, bf16[3584,4096]{1,0:T(8,128)(2,1)} %refs_3_.3, bf16[8,64,4096]{2,1,0:T(8,128)(2,1)} %get-tuple-element.34.refs_4_, ...), custom_call_target="tpu_custom_call" | custom-call | flops 45097156608 | bytes 100663296 | tf_op jit(solution)/shard_map/pallas_call | solution.py:278
  326.8 72.4 %shard_map.126.refs_1_ = bf16[8,64,4096]{2,1,0:T(8,128)(2,1)} custom-call(bf16[8,64,4096]{2,1,0:T(8,128)(2,1)} %get-tuple-element.37.refs_0_, bf16[2,64,4096]{2,1,0:T(8,128)(2,1)} %get-tuple-element.38.refs_1_), custom_call_target="tpu_custom_call" | custom-call | tf_op jit(solution)/shard_map/pallas_call | solution.py:535
  399.1 0.0 copy-start
  399.2 6.7 %shard_map.127 = bf16[1024,4096]{1,0:T(8,128)(2,1)} custom-call(bf16[8,64,4096]{2,1,0:T(8,128)(2,1)} %get-tuple-element.36.refs_0_, bf16[8,64,4096]{2,1,0:T(8,128)(2,1)} %shard_map.126.refs_1_), custom_call_target="tpu_custom_call" | custom-call | bytes 16777216 | tf_op jit(solution)/shard_map/pallas_call | solution.py:561
  405.8 0.0 copy-done
  405.8 0.1 fusion.1
  405.9 0.9 reshape.41
  406.8 0.9 reshape.42
  (2 shorter events, 0.0 us)
Async XLA Ops:
  0.6 3.3 copy-start.1
  39.8 58.0 %copy-start.2 = (bf16[4096]{0:T(1024)(128)(2,1)S(1)}, bf16[4096]{0:T(1024)(128)(2,1)}, u32[]{:S(2)}) copy-start(bf16[4096]{0:T(1024)(128)(2,1)} %param.16) | copy-start | bytes 24580
  399.1 6.7 %copy-start = (bf16[1024,512]{1,0:T(8,128)(2,1)S(1)}, bf16[1024,512]{1,0:T(8,128)(2,1)}, u32[]{:S(2)}) copy-start(bf16[1024,512]{1,0:T(8,128)(2,1)} %get-tuple-element.22.refs_1_) | copy-start | bytes 3145732
